TPU v7x, 32 devices: a whole 2x2x4 slice. The times are simulated.
32 devices in a mesh: grp: 2 (over core), dp: 16 (over z, y, x).
Axes of the slice: x: 2, y: 2, z: 4, core: 2. Of those that a mesh axis runs over, the one named last changes fastest.
Arguments:
- version_tags: int32 [32768], P(('grp', 'dp')), may hold values from 0 to 3
- packed_pos: int32 [32768], P(('grp', 'dp')), may hold values from 0 to 32767, as said below
- valid_mask: int32 [32768, 128], P(('grp', 'dp')), may hold values from 0 to 1, as said below
- returns: float32 [32768, 128], P(('grp', 'dp')), may hold values from -16 to 16
- values: float32 [32768, 128], P(('grp', 'dp')), may hold values from -6 to 6
- log_ratio_new: float32 [32768, 128], P(('grp', 'dp')), may hold values from -4 to 4
- log_ratio_prox: float32 [32768, 128], P(('grp', 'dp')), may hold values from -4 to 4
Outputs:
- token_loss: float32 [32768, 128], P(('grp', 'dp'))
- block_loss: float32 [32768], P(('grp', 'dp'))
Inputs may be any that keep to these rules, and one draw needn't show every extreme that they name: `packed_pos`: A permutation of the blocks. Blocks stay within their group of 16 devices along dp; each device's 1024 packed positions take 1024 // 16 blocks from every device of its group, those of the s-th device of the group at local packed positions s * (64) onward; which of a device's blocks go where is otherwise arbitrary. `valid_mask`: some blocks have no valid token.
All inputs are finite; a program needn't handle non-finite values.
Results may differ from a plain program's by a relative error of at most 0.00002.
Values sent between devices are 32-bit elements; how exact they have to be, the bound alone decides.
A program may use at most 64 MiB of HBM per device.

v0:
```python
import jax
import jax.numpy as jnp
from jax import lax
from jax.sharding import PartitionSpec as P

VERSIONS = 4


def joined(array, axis, combine):
    everything = jax.tree.map(lambda part: lax.all_gather(part, axis), array)
    initial = jax.tree.map(lambda part: part[0], everything)

    def turn(k, so_far):
        return combine(so_far, jax.tree.map(lambda part: part[k], everything))

    return lax.fori_loop(1, lax.axis_size(axis), turn, initial)


def one_hot_of(labels):
    return (labels[:, None] == jnp.arange(VERSIONS)[None, :]).astype(jnp.float32)


def merge_moments(left, right):
    left_count, left_mean, left_sq = left
    right_count, right_mean, right_sq = right
    total_count = left_count + right_count
    delta = right_mean - left_mean
    right_share = right_count / jnp.maximum(total_count, 1.0)
    return (
        total_count,
        left_mean + delta * right_share,
        left_sq + right_sq + delta * delta * left_count * right_share,
    )


def surrogate(prob_ratio, weight, white):
    clipped = jnp.clip(prob_ratio, 0.8, 1.2)
    return -weight * jnp.minimum(prob_ratio * white, clipped * white)


def on_device(version_tags, packed_pos, valid_mask, returns, values, log_ratio_new, log_ratio_prox):
    blk_dev = version_tags.shape[0]
    n_peers = lax.axis_size("dp")
    per_peer = blk_dev // n_peers
    advantage = returns - values
    maskf = valid_mask.astype(jnp.float32)
    onehot = one_hot_of(version_tags)
    block_count = jnp.sum(maskf, axis=1)
    counts = jnp.sum(onehot * block_count[:, None], axis=0)
    adv_sums = jnp.sum(onehot * jnp.sum(maskf * advantage, axis=1)[:, None], axis=0)
    prob_ratio = jnp.exp(log_ratio_new)
    weight = maskf * jnp.exp(log_ratio_prox)
    local_packed = packed_pos % blk_dev
    target = packed_pos // blk_dev % n_peers
    send_index = target * per_peer + local_packed - lax.axis_index("dp") * per_peer

    def place(array):
        return jnp.zeros_like(array).at[send_index].set(array)

    local_mean = adv_sums / jnp.maximum(counts, 1.0)
    centered = advantage - jnp.sum(onehot * local_mean[None, :], axis=1)[:, None]
    local_sq = jnp.sum(onehot * jnp.sum(maskf * centered * centered, axis=1)[:, None], axis=0)
    merged = joined((counts, local_mean, local_sq), "dp", merge_moments)
    total_count, version_mean, squares = joined(merged, "grp", merge_moments)
    version_scale = 1.0 / jnp.sqrt(squares / jnp.maximum(total_count, 1.0) + 0.05)
    block_mean = jnp.sum(onehot * version_mean[None, :], axis=1)
    block_scale = jnp.sum(onehot * version_scale[None, :], axis=1)
    white = (advantage - block_mean[:, None]) * block_scale[:, None]
    local_loss = surrogate(prob_ratio, weight, white)
    local_block = jnp.sum(local_loss, axis=1) / jnp.maximum(block_count, 1.0)
    token_loss, block_loss = (
        lax.all_to_all(place(local_loss), "dp", split_axis=0, concat_axis=0, tiled=True),
        lax.all_to_all(place(local_block), "dp", split_axis=0, concat_axis=0, tiled=True),
    )
    return (token_loss, block_loss)


def solution(mesh):
    in_specs = (
        P(("grp", "dp")),
        P(("grp", "dp")),
        P(("grp", "dp"), None),
        P(("grp", "dp"), None),
        P(("grp", "dp"), None),
        P(("grp", "dp"), None),
        P(("grp", "dp"), None),
    )
    out_specs = (P(("grp", "dp"), None), P(("grp", "dp")))
    return jax.shard_map(
        on_device, mesh=mesh, in_specs=in_specs, out_specs=out_specs, check_vma=False
    )
```

profile of v0, /device:TPU:0, one launch (start us, length us, event | category | flops | bytes accessed | tf_op | source)
XLA Modules:
  0.0 91.4 jit_solution(134701190504602170)
XLA Ops:
  0.6 0.0 copy-start.6
  0.7 0.6 copy-done.6
  1.3 0.6 dynamic-slice
  2.5 0.0 copy-start.3
  2.5 0.0 copy-start
  2.6 1.8 %multiply_reduce_fusion = (f32[1024]{0:T(1024)S(1)}, f32[1024]{0:T(1024)S(1)}, f32[1024,128]{1,0:T(8,128)S(1)}) fusion(s32[1024,128]{1,0:T(8,128)} %param.11, f32[1024,128]{1,0:T(8,128)} %param.12, f32[1024,128]{1,0:T(8,128)} %param.13), kind=kLoop, calls=%fused_computation.17 | loop fusion | flops 653312 | bytes 2105344 | tf_op jit(solution)/shard_map/reduce_sum | solution.py:50
  4.3 0.0 copy-done.3
  4.3 0.2 select_reduce_fusion.4
  4.5 0.1 fusion.23
  4.6 0.1 select_reduce_fusion.3
  4.7 0.0 copy-done
  4.7 0.0 copy-start.1
  4.7 0.0 copy-start.2
  4.7 0.4 fusion.7
  5.1 0.1 select_reduce_fusion.2
  5.2 0.2 dynamic-update-slice
  5.5 0.2 dynamic-update-slice.2
  5.7 43.5 %all-reduce.6 = (f32[64]{0:T(128)S(1)}, f32[64]{0:T(128)S(1)}, f32[64]{0:T(128)S(1)}) all-reduce(f32[64]{0:T(128)S(1)} %dynamic-update-slice, f32[64]{0:T(128)S(1)} %get-tuple-element.238, f32[64]{0:T(128)S(1)} %dynamic-update-slice.2), channel_id=2, replica_groups=mesh['grp'=2,'dp'=16] {'dp'}, use_global_device_ids=true, to_apply=%add | all-reduce | flops 192 | bytes 1536
  49.2 0.1 reshape.45
  49.2 0.1 reshape.46
  49.3 0.1 reshape.66
  49.4 0.0 copy-start.5
  49.4 1.0 %while.12 = (s32[]{:T(128)}, f32[4]{0:T(128)S(1)}, f32[4]{0:T(128)S(1)}, f32[4]{0:T(128)S(1)}, f32[16,4]{1,0:T(8,128)S(1)}, /*index=5*/f32[16,4]{1,0:T(8,128)S(1...) while((s32[]{:T(128)}, f32[4]{0:T(128)S(1)}, f32[4]{0:T(128)S(1)}, f32[4]{0:T(128)S(1)}, ...), condition=%wide.region_8.9_spmd, body=%wide.region_7.8_spmd.sunk | while | flops 53 | bytes 359 | solution.py:16
  50.5 0.0 copy-done.5
  50.5 0.6 dynamic-slice.3
  51.7 0.2 dynamic-update-slice.5
  52.0 0.2 dynamic-update-slice.4
  52.2 0.2 dynamic-update-slice.3
  52.4 2.4 %all-reduce.7 = (f32[8]{0:T(128)S(1)}, f32[8]{0:T(128)S(1)}, f32[8]{0:T(128)S(1)}) all-reduce(f32[8]{0:T(128)S(1)} %dynamic-update-slice.3, f32[8]{0:T(128)S(1)} %dynamic-update-slice.4, f32[8]{0:T(128)S(1)} %dynamic-update-slice.5), channel_id=4, replica_groups=mesh['grp'=2,'dp'=16] {'grp'}, use_global_device_ids=true, to_apply=%add.3 | all-reduce | flops 24 | bytes 192
  54.8 0.1 rsqrt_bitcast_fusion
  54.9 0.1 select_reduce_fusion.1
  55.0 0.0 copy-done.1
  55.0 0.0 copy-done.2
  55.0 0.5 fusion.22
  55.5 0.0 copy-start.4
  55.6 0.7 copy-done.4
  56.2 4.3 %scatter_custom_fusion.1 = f32[1024]{0:T(1024)S(1)} fusion(s32[1024]{0:T(1024)S(1)} %compare_select_fusion, f32[1024]{0:T(1024)S(1)} %maximum_divide_fusion.1, f32[]{:T(128)} %constant.108.clone.1), kind=kCustom, calls=%fused_computation.44 | custom fusion | bytes 4100 | tf_op jit(solution)/shard_map/scatter | solution.py:58
  60.6 0.7 all_to_all.19
  61.2 3.5 %all-to-all-start.1 = ((f32[16,64,1]{1,2,0:T(1,128)}), f32[16,64,1]{1,2,0:T(1,128)S(1)}, u32[]{:S(2)}, u32[]{:S(2)}) async-start(f32[16,64,1]{1,2,0:T(1,128)} %bitcast.14), calls=%async_computation.1 | async-start | bytes 16384 | tf_op jit(solution)/shard_map/all_to_all | solution.py:73
  64.7 3.9 %scatter_custom_fusion = f32[1024,128]{1,0:T(8,128)} fusion(s32[1024]{0:T(1024)S(1)} %compare_select_fusion, f32[1024,128]{1,0:T(8,128)S(1)} %get-tuple-element.237, f32[]{:T(128)} %constant.108.clone.1), kind=kCustom, calls=%fused_computation.19 | custom fusion | bytes 524292 | tf_op jit(solution)/shard_map/scatter | solution.py:58
  68.6 3.4 %all-to-all-done.1 = f32[16,64,1]{1,2,0:T(1,128)S(1)} async-done(((f32[16,64,1]{1,2,0:T(1,128)}), f32[16,64,1]{1,2,0:T(1,128)S(1)}, u32[]{:S(2)}, u32[]{:S(2)}) %all-to-all-start.1) | async-done | bytes 4128 | tf_op jit(solution)/shard_map/all_to_all | solution.py:73
  72.0 3.6 %all-to-all-start = ((f32[16,64,128]{2,1,0:T(8,128)}), f32[16,64,128]{2,1,0:T(8,128)S(1)}, u32[]{:S(2)}, u32[]{:S(2)}) async-start(f32[16,64,128]{2,1,0:T(8,128)} %bitcast.12), calls=%async_computation | async-start | bytes 1048576 | tf_op jit(solution)/shard_map/all_to_all | solution.py:72
  75.6 0.5 broadcast.99
  76.1 0.7 reduce.3
  76.8 0.7 all_to_all.21
  77.4 13.2 %all-to-all-done = f32[16,64,128]{2,1,0:T(8,128)S(1)} async-done(((f32[16,64,128]{2,1,0:T(8,128)}), f32[16,64,128]{2,1,0:T(8,128)S(1)}, u32[]{:S(2)}, u32[]{:S(2)}) %all-to-all-start) | async-done | bytes 524320 | tf_op jit(solution)/shard_map/all_to_all | solution.py:72
  90.6 0.8 copy.32
  (38 shorter events, 0.7 us)
Async XLA Ops:
  0.6 0.7 copy-start.6
  2.5 1.8 %copy-start.3 = (s32[1024]{0:T(1024)S(1)}, s32[1024]{0:T(1024)}, u32[]{:S(2)}) copy-start(s32[1024]{0:T(1024)} %param.9) | copy-start | bytes 12292
  2.5 2.1 %copy-start = (s32[1024,128]{1,0:T(8,128)S(1)}, s32[1024,128]{1,0:T(8,128)}, u32[]{:S(2)}) copy-start(s32[1024,128]{1,0:T(8,128)} %param.11) | copy-start | bytes 1572868
  4.7 50.3 %copy-start.1 = (f32[1024,128]{1,0:T(8,128)S(1)}, f32[1024,128]{1,0:T(8,128)}, u32[]{:S(2)}) copy-start(f32[1024,128]{1,0:T(8,128)} %param.14) | copy-start | bytes 1572868
  4.7 50.3 %copy-start.2 = (f32[1024,128]{1,0:T(8,128)S(1)}, f32[1024,128]{1,0:T(8,128)}, u32[]{:S(2)}) copy-start(f32[1024,128]{1,0:T(8,128)} %param.15) | copy-start | bytes 1572868
  49.4 1.1 %copy-start.5 = (u32[32]{0:T(128)S(1)}, u32[32]{0:T(128)}, u32[]{:S(2)}) copy-start(u32[32]{0:T(128)} %constant.140) | copy-start | bytes 388
  55.5 0.7 copy-start.4
  61.2 10.8 %all-to-all-start.1 = ((f32[16,64,1]{1,2,0:T(1,128)}), f32[16,64,1]{1,2,0:T(1,128)S(1)}, u32[]{:S(2)}, u32[]{:S(2)}) async-start(f32[16,64,1]{1,2,0:T(1,128)} %bitcast.14), calls=%async_computation.1 | async-start | bytes 16384 | tf_op jit(solution)/shard_map/all_to_all | solution.py:73
  72.0 18.6 %all-to-all-start = ((f32[16,64,128]{2,1,0:T(8,128)}), f32[16,64,128]{2,1,0:T(8,128)S(1)}, u32[]{:S(2)}, u32[]{:S(2)}) async-start(f32[16,64,128]{2,1,0:T(8,128)} %bitcast.12), calls=%async_computation | async-start | bytes 1048576 | tf_op jit(solution)/shard_map/all_to_all | solution.py:72
where the time goes:
time: 91.8 us; the launch traced here: 91.4 us
  blocking collectives  45.9 us (50%)
  waiting for transfers between devices  16.6 us (18%)
  local copies, waits for them, and re-layouts  14.7 us (16%)
  starting transfers between devices  7.07 us (8%)
  other arithmetic  4.68 us (5%)
  between operations  2.14 us (2%)
    unnamed x2, blocking collectives  45.9 us
    all_to_all x1, waiting for transfers between devices, on_device(): lax.all_to_all(place(local_loss), 'dp', split_axis=0, concat_axis=0, tile...  13.2 us
    scatter x2, local copies, waits for them, and re-layouts, place(): return jnp.zeros_like(array).at[send_index].set(array)  8.17 us
    unnamed x28, local copies, waits for them, and re-layouts  4.41 us
    all_to_all x1, starting transfers between devices, on_device(): lax.all_to_all(place(local_loss), 'dp', split_axis=0, concat_axis=0, tile...  3.57 us
    all_to_all x1, starting transfers between devices, on_device(): lax.all_to_all(place(local_block), 'dp', split_axis=0, concat_axis=0, til...  3.49 us
    all_to_all x1, waiting for transfers between devices, on_device(): lax.all_to_all(place(local_block), 'dp', split_axis=0, concat_axis=0, til...  3.4 us
    all_to_all x3, local copies, waits for them, and re-layouts, on_device(): lax.all_to_all(place(local_block), 'dp', split_axis=0, concat_axis=0, til...  1.84 us
  transfers between devices with their start and end apart: 2, of which 2 were waited for; matrix products, arithmetic and copies ran while one was open for 6% of the time, Pallas kernels for 0%

commit v1 on v0

v1 whole, which is shorter than its diff:
```python
import functools

import jax
import jax.numpy as jnp
from jax import lax
from jax.experimental import pallas as pl
from jax.experimental.pallas import tpu as pltpu
from jax.sharding import PartitionSpec as P

VERSIONS = 4
LANES = 128
F32 = jnp.float32
BF16 = jnp.bfloat16
MESH = pl.DeviceIdType.MESH
NT = (((1,), (1,)), ((), ()))


def fold(array):
    return jnp.sum(array.reshape(-1, 8, array.shape[-1]), axis=0)


def total(array):
    return jnp.sum(jnp.sum(array, axis=0, keepdims=True), axis=1, keepdims=True)


def pick(tags, per_version):
    chosen = per_version[-1]
    for v in range(VERSIONS - 2, -1, -1):
        chosen = jnp.where(tags == v, per_version[v], chosen)
    return chosen


def kernel(
    n_grp, n_dp,
    tags_ref, packed_ref, mask_hbm, ret_hbm, val_hbm, new_hbm, prox_hbm,
    tok_out, blk_out,
    mask_s, ret_s, val_s, new_s, prox_s, tags_s, perm_s, split_s, send_s, bsend_s, stats_s,
    load_sem, st_send, st_recv, tok_send, tok_recv, blk_send, blk_recv, own_sem,
):
    n_all = n_grp * n_dp
    my_grp, my_dp = lax.axis_index("grp"), lax.axis_index("dp")
    me = my_grp * n_dp + my_dp
    rows = ret_s.shape[0]
    tiles = rows // LANES
    per_peer = rows // n_dp
    group = max(1, 256 // per_peer)
    chunk = group * per_peer
    n_chunks = rows // chunk

    def device(index):
        return {"grp": index // n_dp, "dp": lax.rem(index, n_dp)}

    loads = [
        pltpu.make_async_copy(src, dst, load_sem.at[i])
        for i, (src, dst) in enumerate(
            ((ret_hbm, ret_s), (val_hbm, val_s), (mask_hbm, mask_s), (new_hbm, new_s), (prox_hbm, prox_s))
        )
    ]
    for load in loads:
        load.start()

    barrier = pltpu.get_barrier_semaphore()

    @pl.loop(1, n_all)
    def _(k):
        pl.semaphore_signal(
            barrier, inc=1, device_id=device(lax.rem(me + k, n_all)), device_id_type=MESH
        )

    eye = lax.broadcasted_iota(jnp.int32, (LANES, LANES), 0) == lax.broadcasted_iota(
        jnp.int32, (LANES, LANES), 1
    )
    ones = jnp.ones((LANES, LANES), BF16)
    for t in range(tiles):
        row = tags_ref[t : t + 1, :].astype(F32)
        spread = jnp.where(eye, jnp.broadcast_to(row, (LANES, LANES)), 0.0).astype(BF16)
        tags_s[t * LANES : (t + 1) * LANES, :] = jnp.dot(spread, ones, preferred_element_type=F32)

    for load in loads[:3]:
        load.wait()
    counts = [jnp.zeros((8, LANES), F32)] * VERSIONS
    sums = [jnp.zeros((8, LANES), F32)] * VERSIONS
    for t in range(tiles):
        at = slice(t * LANES, (t + 1) * LANES)
        maskf = mask_s[at, :].astype(F32)
        advantage = ret_s[at, :] - val_s[at, :]
        ret_s[at, :] = advantage
        tags = tags_s[at, :]
        for v in range(VERSIONS):
            valid = jnp.where(tags == v, maskf, 0.0)
            counts[v] = counts[v] + fold(valid)
            sums[v] = sums[v] + fold(valid * advantage)
    counts = [total(c) for c in counts]
    means = [total(s) / jnp.maximum(c, 1.0) for s, c in zip(sums, counts)]
    squares = [jnp.zeros((8, LANES), F32)] * VERSIONS
    for t in range(tiles):
        at = slice(t * LANES, (t + 1) * LANES)
        tags = tags_s[at, :]
        centered = ret_s[at, :] - pick(tags, means)
        square = mask_s[at, :].astype(F32) * centered * centered
        for v in range(VERSIONS):
            squares[v] = squares[v] + fold(jnp.where(tags == v, square, 0.0))
    squares = [total(s) for s in squares]
    lane = lax.broadcasted_iota(jnp.int32, (1, LANES), 1)
    message = jnp.zeros((1, LANES), F32)
    for i, value in enumerate(counts + means + squares):
        message = jnp.where(lane == i, value, message)
    stats_s[me] = message

    pl.semaphore_wait(barrier, n_all - 1)

    @pl.loop(1, n_all)
    def _(k):
        pltpu.make_async_remote_copy(
            src_ref=stats_s.at[me], dst_ref=stats_s.at[me], send_sem=st_send, recv_sem=st_recv,
            device_id=device(lax.rem(me + k, n_all)), device_id_type=MESH,
        ).start()

    base = my_grp * (rows * n_dp) + my_dp * per_peer
    for c in range(n_chunks):
        slot = lax.broadcasted_iota(jnp.int32, (chunk, LANES), 0)
        want = base + (slot // per_peer + c * group) * rows + lax.rem(slot, per_peer)
        for t in range(tiles):
            hit = want == packed_ref[t : t + 1, :]
            perm_s[c * chunk : (c + 1) * chunk, t * LANES : (t + 1) * LANES] = (
                jnp.where(hit, 1.0, 0.0).astype(BF16)
            )
    for load in loads[3:]:
        load.wait()
    block_counts = []
    for t in range(tiles):
        at = slice(t * LANES, (t + 1) * LANES)
        maskf = mask_s[at, :].astype(F32)
        weight = -maskf * jnp.exp(prox_s[at, :])
        ratio = jnp.exp(new_s[at, :])
        new_s[at, :] = weight * ratio
        prox_s[at, :] = weight * jnp.clip(ratio, 0.8, 1.2)
        block_counts.append(
            lax.dot_general(ones[:8], maskf.astype(BF16), NT, preferred_element_type=F32)
        )

    everyone = stats_s.at[pl.ds(0, n_all - 1)]
    pltpu.make_async_copy(everyone, everyone, st_recv).wait()
    every_count = stats_s[...]
    every_mean = pltpu.roll(every_count, LANES - VERSIONS, 2)
    every_square = pltpu.roll(every_count, LANES - 2 * VERSIONS, 2)
    total_count = jnp.maximum(jnp.sum(every_count, axis=0), 1.0)
    mean_row = jnp.sum(every_count * every_mean, axis=0) / total_count
    off = every_mean - mean_row[None]
    square_row = jnp.sum(every_square + every_count * off * off, axis=0)
    scale_row = 1.0 / jnp.sqrt(square_row / total_count + 0.05)
    means = [mean_row[:, v : v + 1] for v in range(VERSIONS)]
    scales = [scale_row[:, v : v + 1] for v in range(VERSIONS)]

    for t in range(tiles):
        at = slice(t * LANES, (t + 1) * LANES)
        tags = tags_s[at, :]
        white = (ret_s[at, :] - pick(tags, means)) * pick(tags, scales)
        loss = jnp.maximum(new_s[at, :] * white, prox_s[at, :] * white)
        high = loss.astype(BF16)
        split_s[at, :LANES] = high
        split_s[at, LANES:] = (loss - high.astype(F32)).astype(BF16)

    my_chunk = my_dp // group
    for i in range(n_chunks):
        c = lax.rem(my_chunk + i, n_chunks)
        at = pl.ds(pl.multiple_of(c * chunk, chunk), chunk)
        parts = jnp.dot(perm_s[at, :], split_s[...], preferred_element_type=F32)
        send_s[at, :] = parts[:, :LANES] + parts[:, LANES:]
        for q in range(group):
            peer = c * group + q
            src = send_s.at[pl.ds(pl.multiple_of(peer * per_peer, per_peer), per_peer)]
            dst = tok_out.at[pl.ds(pl.multiple_of(my_dp * per_peer, per_peer), per_peer)]

            @pl.when(peer != my_dp)
            def _():
                pltpu.make_async_remote_copy(
                    src_ref=src, dst_ref=dst, send_sem=tok_send, recv_sem=tok_recv,
                    device_id={"grp": my_grp, "dp": peer}, device_id_type=MESH,
                ).start()

            @pl.when(peer == my_dp)
            def _():
                pltpu.make_async_copy(src, dst, own_sem).start()

    sub = lax.broadcasted_iota(jnp.int32, (8, LANES), 0)
    pieces = []
    for t in range(tiles):
        at = slice(t * LANES, (t + 1) * LANES)
        block = lax.dot_general(
            jnp.ones((8, 2 * LANES), BF16), split_s[at, :], NT, preferred_element_type=F32
        ) / jnp.maximum(block_counts[t], 1.0)
        high = block.astype(BF16).astype(F32)
        middle = (block - high).astype(BF16).astype(F32)
        low = block - high - middle
        piece = jnp.where(sub == 0, high, jnp.where(sub == 1, middle, jnp.where(sub == 2, low, 0.0)))
        pieces.append(piece.astype(BF16))
    blocks = jnp.concatenate(pieces, axis=1)
    for i in range(n_chunks):
        c = lax.rem(my_chunk + i, n_chunks)
        at = pl.ds(pl.multiple_of(c * chunk, chunk), chunk)
        moved = jnp.sum(
            lax.dot_general(blocks, perm_s[at, :], NT, preferred_element_type=F32), axis=0, keepdims=True
        )
        for q in range(group):
            peer = c * group + q
            part = moved[:, q * per_peer : (q + 1) * per_peer]
            bsend_s[peer] = part

            @pl.when(peer != my_dp)
            def _():
                pltpu.make_async_remote_copy(
                    src_ref=bsend_s.at[peer], dst_ref=blk_out.at[my_dp], send_sem=blk_send,
                    recv_sem=blk_recv, device_id={"grp": my_grp, "dp": peer}, device_id_type=MESH,
                ).start()

            @pl.when(peer == my_dp)
            def _():
                blk_out[my_dp] = part

    own = send_s.at[pl.ds(0, per_peer)]
    pltpu.make_async_copy(own, tok_out.at[pl.ds(0, per_peer)], own_sem).wait()
    pltpu.make_async_copy(everyone, everyone, st_send).wait()
    others = pl.ds(0, rows - per_peer)
    for sem in (tok_send, tok_recv):
        pltpu.make_async_copy(send_s.at[others], tok_out.at[others], sem).wait()
    peers = bsend_s.at[pl.ds(0, n_dp - 1)]
    for sem in (blk_send, blk_recv):
        pltpu.make_async_copy(peers, peers, sem).wait()


def solution(mesh):
    n_grp, n_dp = mesh.shape["grp"], mesh.shape["dp"]

    def on_device(version_tags, packed_pos, valid_mask, returns, values, log_ratio_new, log_ratio_prox):
        rows, width = returns.shape
        n_all = n_grp * n_dp
        per_peer = rows // n_dp
        vmem = pl.BlockSpec(memory_space=pltpu.VMEM)
        anywhere = pl.BlockSpec(memory_space=pl.ANY)
        dma = pltpu.SemaphoreType.DMA
        full = pltpu.VMEM((rows, width), F32)
        token_loss, block_loss = pl.pallas_call(
            functools.partial(kernel, n_grp, n_dp),
            out_shape=(
                jax.ShapeDtypeStruct((rows, width), F32),
                jax.ShapeDtypeStruct((n_dp, 1, per_peer), F32),
            ),
            in_specs=[vmem, vmem] + [anywhere] * 5,
            out_specs=(anywhere, vmem),
            scratch_shapes=[
                pltpu.VMEM((rows, width), jnp.int32), full, full, full, full, full,
                pltpu.VMEM((rows, rows), BF16),
                pltpu.VMEM((rows, 2 * width), BF16),
                full,
                pltpu.VMEM((n_dp, 1, per_peer), F32),
                pltpu.VMEM((n_all, 1, width), F32),
                dma((5,)), dma, dma, dma, dma, dma, dma, dma,
            ],
            compiler_params=pltpu.CompilerParams(collective_id=0, has_side_effects=True),
        )(
            version_tags.reshape(rows // LANES, LANES), packed_pos.reshape(rows // LANES, LANES),
            valid_mask, returns, values, log_ratio_new, log_ratio_prox,
        )
        return token_loss, block_loss.reshape(rows)

    each = P(("grp", "dp"))
    wide = P(("grp", "dp"), None)
    return jax.shard_map(
        on_device, mesh=mesh, in_specs=(each, each) + (wide,) * 5, out_specs=(wide, each), check_vma=False
    )
```

time: 91.8 us -> 34.1 us (0.37)
  blocking collectives: 45.9 us -> 0 us
  Pallas kernels: 0 us -> 28.8 us
  waiting for transfers between devices: 16.6 us -> 0 us
  local copies, waits for them, and re-layouts: 14.7 us -> 3.04 us
  starting transfers between devices: 7.07 us -> 0 us
  other arithmetic: 4.68 us -> 1.37 us
  between operations: 2.14 us -> 0.64 us
    unnamed x2 -> x0, blocking collectives: 45.9 us -> none
    pallas_call x0 -> x1, Pallas kernels: none -> 28.8 us  [on_device(): pl.pallas_call(functools.partial(kernel, n_grp, n_dp), out_shape=(jax.Sha...]
    all_to_all x2 -> x0, waiting for transfers between devices: 16.6 us -> none  [the longest x1 13.2 us: on_device(): lax.all_to_all(place(local_loss), 'dp', split_axis=0, concat_axis=0, tile...]
    scatter x2 -> x0, local copies, waits for them, and re-layouts: 8.17 us -> none  [place(): return jnp.zeros_like(array).at[send_index].set(array)]
    all_to_all x2 -> x0, starting transfers between devices: 7.07 us -> none  [the longest x1 3.57 us: on_device(): lax.all_to_all(place(local_loss), 'dp', split_axis=0, concat_axis=0, tile...]
    reduce_sum x7 -> x0, other arithmetic: 3.08 us -> none  [the longest x1 1.77 us: on_device(): jnp.sum(maskf * advantage, axis=1)[:, None]]
    unnamed x28 -> x1, local copies, waits for them, and re-layouts: 4.41 us -> 1.87 us
    all_to_all x3 -> x0, local copies, waits for them, and re-layouts: 1.84 us -> none  [on_device(): lax.all_to_all(place(local_block), 'dp', split_axis=0, concat_axis=0, til...]
  transfers between devices with their start and end apart: 2 -> 0, of which waited for: 2 -> 0; matrix products, arithmetic and copies ran while one was open for 6% -> 0% of each run, Pallas kernels for 0% -> 0%
where the time goes in v1:
time: 34.1 us; the launch traced here: 33.9 us
  Pallas kernels  28.8 us (84%)
  local copies, waits for them, and re-layouts  3.04 us (9%)
  other arithmetic  1.37 us (4%)
  between operations  0.64 us (2%)
    pallas_call x1, Pallas kernels, on_device(): pl.pallas_call(functools.partial(kernel, n_grp, n_dp), out_shape=(jax.Sha...  28.8 us
    unnamed x1, local copies, waits for them, and re-layouts  1.87 us
    pallas_call x1, other arithmetic, on_device(): pl.pallas_call(functools.partial(kernel, n_grp, n_dp), out_shape=(jax.Sha...  1.37 us

profile of v1, /device:TPU:0, one launch (start us, length us, event | category | flops | bytes accessed | tf_op | source)
XLA Modules:
  0.0 33.9 jit_solution(14112102069406060600)
XLA Ops:
  0.6 28.8 %shard_map.86 = (f32[1024,128]{1,0:T(8,128)}, f32[16,1,64]{2,1,0:T(1,128)}) custom-call(s32[8,128]{1,0:T(8,128)} %bitcast.2, s32[8,128]{1,0:T(8,128)} %bitcast.3, s32[1024,128]{1,0:T(8,128)} %mask_hbm.1, f32[1024,128]{1,0:T(8,128)} %ret_hbm.1, f32[1024,128]{1,0:T(8,128)} %val_hbm.1, f32[1024,128]{1,0:T(8,128)} %new_hbm.1, f32[1024,128]{1,0:T(8,128)} %prox_hbm.1), custom_call_target="tpu_custom_call" | custom-call | tf_op jit(solution)/shard_map/pallas_call | solution.py:243
  29.4 0.5 %broadcast.3 = f32[]{:T(128)} broadcast(f32[]{:T(128)} %constant.3), dimensions={} | broadcast | bytes 8 | tf_op jit(solution)/shard_map/pallas_call | solution.py:243
  30.0 1.4 %reduce.3 = f32[16,64]{1,0:T(8,128)S(1)} reduce(f32[16,1,64]{2,1,0:T(1,128)} %get-tuple-element.5, f32[]{:T(128)} %broadcast.3), dimensions={1}, to_apply=%get-tuple-element.5.reduce_sub_computation.3 | reduce | bytes 8196 | tf_op jit(solution)/shard_map/pallas_call | solution.py:243
  31.3 0.7 %reshape.15 = f32[1024]{0:T(1024)} reshape(f32[16,64]{1,0:T(8,128)S(1)} %reduce.3) | data formatting | bytes 8192 | tf_op jit(solution)/shard_map/reshape | solution.py:265
  32.0 1.9 %copy.10 = f32[1024,128]{1,0:T(8,128)} copy(f32[1024,128]{1,0:T(8,128)} %get-tuple-element.8) | data formatting | bytes 1048576

commit v2 on v1

--- a/solution.py
+++ b/solution.py
@@ -34,7 +34,7 @@
     n_grp, n_dp,
     tags_ref, packed_ref, mask_hbm, ret_hbm, val_hbm, new_hbm, prox_hbm,
     tok_out, blk_out,
-    mask_s, ret_s, val_s, new_s, prox_s, tags_s, perm_s, split_s, send_s, bsend_s, stats_s,
+    mask_s, ret_s, val_s, new_s, prox_s, tags_s, perm_s, split_s, send_s, bsend_s, brecv_s, stats_s,
     load_sem, st_send, st_recv, tok_send, tok_recv, blk_send, blk_recv, own_sem,
 ):
     n_all = n_grp * n_dp
@@ -205,18 +205,20 @@
         for q in range(group):
             peer = c * group + q
             part = moved[:, q * per_peer : (q + 1) * per_peer]
-            bsend_s[peer] = part
+            bsend_s[peer] = jnp.concatenate(
+                [part, jnp.zeros((1, LANES - per_peer), F32)], axis=1
+            )
 
             @pl.when(peer != my_dp)
             def _():
                 pltpu.make_async_remote_copy(
-                    src_ref=bsend_s.at[peer], dst_ref=blk_out.at[my_dp], send_sem=blk_send,
+                    src_ref=bsend_s.at[peer], dst_ref=brecv_s.at[my_dp], send_sem=blk_send,
                     recv_sem=blk_recv, device_id={"grp": my_grp, "dp": peer}, device_id_type=MESH,
                 ).start()
 
             @pl.when(peer == my_dp)
             def _():
-                blk_out[my_dp] = part
+                brecv_s[my_dp] = bsend_s[peer]
 
     own = send_s.at[pl.ds(0, per_peer)]
     pltpu.make_async_copy(own, tok_out.at[pl.ds(0, per_peer)], own_sem).wait()
@@ -227,6 +229,12 @@
     peers = bsend_s.at[pl.ds(0, n_dp - 1)]
     for sem in (blk_send, blk_recv):
         pltpu.make_async_copy(peers, peers, sem).wait()
+    beside = LANES // per_peer
+    for r in range(tiles):
+        line = brecv_s[r * beside]
+        for q in range(1, beside):
+            line = line + pltpu.roll(brecv_s[r * beside + q], q * per_peer, 1)
+        blk_out[r : r + 1, :] = line
 
 
 def solution(mesh):
@@ -243,17 +251,18 @@
         token_loss, block_loss = pl.pallas_call(
             functools.partial(kernel, n_grp, n_dp),
             out_shape=(
-                jax.ShapeDtypeStruct((rows, width), F32),
-                jax.ShapeDtypeStruct((n_dp, 1, per_peer), F32),
+                pltpu.VMEM((rows, width), F32),
+                pltpu.VMEM((rows // LANES, LANES), F32),
             ),
             in_specs=[vmem, vmem] + [anywhere] * 5,
-            out_specs=(anywhere, vmem),
+            out_specs=(vmem, vmem),
             scratch_shapes=[
                 pltpu.VMEM((rows, width), jnp.int32), full, full, full, full, full,
                 pltpu.VMEM((rows, rows), BF16),
                 pltpu.VMEM((rows, 2 * width), BF16),
                 full,
-                pltpu.VMEM((n_dp, 1, per_peer), F32),
+                pltpu.VMEM((n_dp, 1, width), F32),
+                pltpu.VMEM((n_dp, 1, width), F32),
                 pltpu.VMEM((n_all, 1, width), F32),
                 dma((5,)), dma, dma, dma, dma, dma, dma, dma,
             ],

time: 34.1 us -> 30.6 us (0.90)
  local copies, waits for them, and re-layouts: 3.04 us -> 1.39 us
  other arithmetic: 1.37 us -> 0 us
  Pallas kernels: 28.8 us -> 28.3 us
    pallas_call x1 -> x0, other arithmetic: 1.37 us -> none  [on_device(): pl.pallas_call(functools.partial(kernel, n_grp, n_dp), out_shape=(jax.Sha...]
    reshape x1 -> x0, local copies, waits for them, and re-layouts: 0.66 us -> none  [on_device(): return (token_loss, block_loss.reshape(rows))]
    pallas_call x1 -> x0, local copies, waits for them, and re-layouts: 0.51 us -> none  [on_device(): pl.pallas_call(functools.partial(kernel, n_grp, n_dp), out_shape=(jax.Sha...]
    unnamed x1 -> x2, local copies, waits for them, and re-layouts: 1.87 us -> 1.39 us
    pallas_call x1, Pallas kernels: 28.8 us -> 28.3 us  [on_device(): pl.pallas_call(functools.partial(kernel, n_grp, n_dp), out_shape=(pltpu.V...]
where the time goes in v2:
time: 30.6 us; the launch traced here: 30.4 us
  Pallas kernels  28.3 us (92%)
  local copies, waits for them, and re-layouts  1.39 us (5%)
  between operations  0.64 us (2%)
    pallas_call x1, Pallas kernels, on_device(): pl.pallas_call(functools.partial(kernel, n_grp, n_dp), out_shape=(pltpu.V...  28.3 us
    unnamed x2, local copies, waits for them, and re-layouts  1.39 us

profile of v2, /device:TPU:0, one launch (start us, length us, event | category | flops | bytes accessed | tf_op | source)
XLA Modules:
  0.0 30.4 jit_solution(8977907259248678106)
XLA Ops:
  0.6 28.3 %shard_map.86 = (f32[1024,128]{1,0:T(8,128)S(1)}, f32[8,128]{1,0:T(8,128)S(1)}) custom-call(s32[8,128]{1,0:T(8,128)} %bitcast.4, s32[8,128]{1,0:T(8,128)} %bitcast.5, s32[1024,128]{1,0:T(8,128)} %mask_hbm.1, f32[1024,128]{1,0:T(8,128)} %ret_hbm.1, f32[1024,128]{1,0:T(8,128)} %val_hbm.1, f32[1024,128]{1,0:T(8,128)} %new_hbm.1, f32[1024,128]{1,0:T(8,128)} %prox_hbm.1), custom_call_target="tpu_custom_call" | custom-call | tf_op jit(solution)/shard_map/pallas_call | solution.py:251
  29.0 0.8 %copy.11 = f32[1024,128]{1,0:T(8,128)} copy(f32[1024,128]{1,0:T(8,128)S(1)} %get-tuple-element.6) | data formatting | bytes 1048576
  29.8 0.6 %copy.12 = f32[1024]{0:T(1024)} copy(f32[1024]{0:T(1024)S(1)} %bitcast.3) | data formatting | bytes 8192

commit v3 on v2

--- a/solution.py
+++ b/solution.py
@@ -61,7 +61,7 @@
 
     barrier = pltpu.get_barrier_semaphore()
 
-    @pl.loop(1, n_all)
+    @pl.loop(1, n_all, unroll=n_all <= 64)
     def _(k):
         pl.semaphore_signal(
             barrier, inc=1, device_id=device(lax.rem(me + k, n_all)), device_id_type=MESH
@@ -109,7 +109,7 @@
 
     pl.semaphore_wait(barrier, n_all - 1)
 
-    @pl.loop(1, n_all)
+    @pl.loop(1, n_all, unroll=n_all <= 64)
     def _(k):
         pltpu.make_async_remote_copy(
             src_ref=stats_s.at[me], dst_ref=stats_s.at[me], send_sem=st_send, recv_sem=st_recv,
@@ -163,7 +163,7 @@
 
     my_chunk = my_dp // group
     for i in range(n_chunks):
-        c = lax.rem(my_chunk + i, n_chunks)
+        c = jnp.where(my_chunk < n_chunks // 2, n_chunks - 1 - i, i)
         at = pl.ds(pl.multiple_of(c * chunk, chunk), chunk)
         parts = jnp.dot(perm_s[at, :], split_s[...], preferred_element_type=F32)
         send_s[at, :] = parts[:, :LANES] + parts[:, LANES:]
@@ -197,7 +197,7 @@
         pieces.append(piece.astype(BF16))
     blocks = jnp.concatenate(pieces, axis=1)
     for i in range(n_chunks):
-        c = lax.rem(my_chunk + i, n_chunks)
+        c = jnp.where(my_chunk < n_chunks // 2, n_chunks - 1 - i, i)
         at = pl.ds(pl.multiple_of(c * chunk, chunk), chunk)
         moved = jnp.sum(
             lax.dot_general(blocks, perm_s[at, :], NT, preferred_element_type=F32), axis=0, keepdims=True
@@ -235,6 +235,17 @@
         for q in range(1, beside):
             line = line + pltpu.roll(brecv_s[r * beside + q], q * per_peer, 1)
         blk_out[r : r + 1, :] = line
+
+
+def finish(tok_ref, blk_ref, tok_out, blk_out, sem):
+    copies = [
+        pltpu.make_async_copy(tok_ref, tok_out, sem.at[0]),
+        pltpu.make_async_copy(blk_ref, blk_out, sem.at[1]),
+    ]
+    for copy in copies:
+        copy.start()
+    for copy in copies:
+        copy.wait()
 
 
 def solution(mesh):
@@ -271,6 +282,17 @@
             version_tags.reshape(rows // LANES, LANES), packed_pos.reshape(rows // LANES, LANES),
             valid_mask, returns, values, log_ratio_new, log_ratio_prox,
         )
+        token_loss, block_loss = pl.pallas_call(
+            finish,
+            out_shape=(
+                jax.ShapeDtypeStruct((rows, width), F32),
+                jax.ShapeDtypeStruct((rows // LANES, LANES), F32),
+            ),
+            in_specs=[anywhere] * 2,
+            out_specs=(anywhere, anywhere),
+            scratch_shapes=[dma((2,))],
+            compiler_params=pltpu.CompilerParams(vmem_limit_bytes=1 << 20),
+        )(token_loss, block_loss)
         return token_loss, block_loss.reshape(rows)
 
     each = P(("grp", "dp"))

time: 30.6 us -> 28.9 us (0.944)
  local copies, waits for them, and re-layouts: 1.39 us -> 0 us
    unnamed x2 -> x0, local copies, waits for them, and re-layouts: 1.39 us -> none
    pallas_call x1, Pallas kernels: 28.3 us -> 27.3 us  [on_device(): pl.pallas_call(functools.partial(kernel, n_grp, n_dp), out_shape=(pltpu.V...]
    pallas_call x0 -> x1, Pallas kernels: none -> 0.81 us  [on_device(): pl.pallas_call(finish, out_shape=(jax.ShapeDtypeStruct((rows, width), F32...]
where the time goes in v3:
time: 28.9 us; the launch traced here: 28.7 us
  Pallas kernels  28.1 us (97%)
  between operations  0.64 us (2%)
    pallas_call x1, Pallas kernels, on_device(): pl.pallas_call(functools.partial(kernel, n_grp, n_dp), out_shape=(pltpu.V...  27.3 us
    pallas_call x1, Pallas kernels, on_device(): pl.pallas_call(finish, out_shape=(jax.ShapeDtypeStruct((rows, width), F32...  0.81 us

profile of v3, /device:TPU:0, one launch (start us, length us, event | category | flops | bytes accessed | tf_op | source)
XLA Modules:
  0.0 28.7 jit_solution(9862221135093626910)
XLA Ops:
  0.6 27.3 %shard_map.86 = (f32[1024,128]{1,0:T(8,128)S(1)}, f32[8,128]{1,0:T(8,128)S(1)}) custom-call(s32[8,128]{1,0:T(8,128)} %bitcast.3, s32[8,128]{1,0:T(8,128)} %bitcast.4, s32[1024,128]{1,0:T(8,128)} %mask_hbm.1, f32[1024,128]{1,0:T(8,128)} %ret_hbm.1, f32[1024,128]{1,0:T(8,128)} %val_hbm.1, f32[1024,128]{1,0:T(8,128)} %new_hbm.1, f32[1024,128]{1,0:T(8,128)} %prox_hbm.1), custom_call_target="tpu_custom_call" | custom-call | tf_op jit(solution)/shard_map/pallas_call | solution.py:262
  27.9 0.8 %shard_map.87 = (f32[1024,128]{1,0:T(8,128)}, f32[8,128]{1,0:T(8,128)}) custom-call(f32[1024,128]{1,0:T(8,128)S(1)} %get-tuple-element.6.tok_ref, f32[8,128]{1,0:T(8,128)S(1)} %get-tuple-element.7.blk_ref), custom_call_target="tpu_custom_call" | custom-call | tf_op jit(solution)/shard_map/pallas_call | solution.py:285

commit v4 on v3

--- a/solution.py
+++ b/solution.py
@@ -47,8 +47,22 @@
     chunk = group * per_peer
     n_chunks = rows // chunk
 
-    def device(index):
-        return {"grp": index // n_dp, "dp": lax.rem(index, n_dp)}
+    place = my_dp * n_grp + my_grp
+    low = place < n_all // 2
+    mirror = jnp.where(low, n_all - 1 - place, place)
+
+    def device(k):
+        step = k - 1 + (k > mirror).astype(jnp.int32)
+        index = jnp.where(low, n_all - 1 - step, step)
+        return {"grp": lax.rem(index, n_grp), "dp": index // n_grp}
+
+    barrier = pltpu.get_barrier_semaphore()
+
+    @pl.loop(1, n_all, unroll=n_all <= 64)
+    def _(k):
+        pl.semaphore_signal(
+            barrier, inc=1, device_id=device(k), device_id_type=MESH
+        )
 
     loads = [
         pltpu.make_async_copy(src, dst, load_sem.at[i])
@@ -56,16 +70,8 @@
             ((ret_hbm, ret_s), (val_hbm, val_s), (mask_hbm, mask_s), (new_hbm, new_s), (prox_hbm, prox_s))
         )
     ]
-    for load in loads:
+    for load in loads[:3]:
         load.start()
-
-    barrier = pltpu.get_barrier_semaphore()
-
-    @pl.loop(1, n_all, unroll=n_all <= 64)
-    def _(k):
-        pl.semaphore_signal(
-            barrier, inc=1, device_id=device(lax.rem(me + k, n_all)), device_id_type=MESH
-        )
 
     eye = lax.broadcasted_iota(jnp.int32, (LANES, LANES), 0) == lax.broadcasted_iota(
         jnp.int32, (LANES, LANES), 1
@@ -78,28 +84,30 @@
 
     for load in loads[:3]:
         load.wait()
+    for load in loads[3:]:
+        load.start()
     counts = [jnp.zeros((8, LANES), F32)] * VERSIONS
     sums = [jnp.zeros((8, LANES), F32)] * VERSIONS
     for t in range(tiles):
         at = slice(t * LANES, (t + 1) * LANES)
-        maskf = mask_s[at, :].astype(F32)
         advantage = ret_s[at, :] - val_s[at, :]
         ret_s[at, :] = advantage
-        tags = tags_s[at, :]
+        marked = jnp.where(mask_s[at, :] == 0, -1.0, tags_s[at, :])
+        val_s[at, :] = marked
         for v in range(VERSIONS):
-            valid = jnp.where(tags == v, maskf, 0.0)
-            counts[v] = counts[v] + fold(valid)
-            sums[v] = sums[v] + fold(valid * advantage)
+            valid = marked == v
+            counts[v] = counts[v] + fold(jnp.where(valid, 1.0, 0.0))
+            sums[v] = sums[v] + fold(jnp.where(valid, advantage, 0.0))
     counts = [total(c) for c in counts]
     means = [total(s) / jnp.maximum(c, 1.0) for s, c in zip(sums, counts)]
     squares = [jnp.zeros((8, LANES), F32)] * VERSIONS
     for t in range(tiles):
         at = slice(t * LANES, (t + 1) * LANES)
-        tags = tags_s[at, :]
-        centered = ret_s[at, :] - pick(tags, means)
-        square = mask_s[at, :].astype(F32) * centered * centered
+        marked = val_s[at, :]
+        advantage = ret_s[at, :]
         for v in range(VERSIONS):
-            squares[v] = squares[v] + fold(jnp.where(tags == v, square, 0.0))
+            centered = jnp.where(marked == v, advantage - means[v], 0.0)
+            squares[v] = squares[v] + fold(centered * centered)
     squares = [total(s) for s in squares]
     lane = lax.broadcasted_iota(jnp.int32, (1, LANES), 1)
     message = jnp.zeros((1, LANES), F32)
@@ -113,7 +121,7 @@
     def _(k):
         pltpu.make_async_remote_copy(
             src_ref=stats_s.at[me], dst_ref=stats_s.at[me], send_sem=st_send, recv_sem=st_recv,
-            device_id=device(lax.rem(me + k, n_all)), device_id_type=MESH,
+            device_id=device(k), device_id_type=MESH,
         ).start()
 
     base = my_grp * (rows * n_dp) + my_dp * per_peer
@@ -139,6 +147,30 @@
             lax.dot_general(ones[:8], maskf.astype(BF16), NT, preferred_element_type=F32)
         )
 
+    my_chunk = my_dp // group
+    blocks = jnp.concatenate(block_counts, axis=1).astype(BF16)
+    for i in range(n_chunks):
+        c = jnp.where(my_chunk < n_chunks // 2, n_chunks - 1 - i, i)
+        at = pl.ds(pl.multiple_of(c * chunk, chunk), chunk)
+        moved = lax.dot_general(blocks, perm_s[at, :], NT, preferred_element_type=F32)[:1]
+        for q in range(group):
+            peer = c * group + q
+            part = moved[:, q * per_peer : (q + 1) * per_peer]
+            bsend_s[peer] = jnp.concatenate(
+                [part, jnp.zeros((1, LANES - per_peer), F32)], axis=1
+            )
+
+            @pl.when(peer != my_dp)
+            def _():
+                pltpu.make_async_remote_copy(
+                    src_ref=bsend_s.at[peer], dst_ref=brecv_s.at[my_dp], send_sem=blk_send,
+                    recv_sem=blk_recv, device_id={"grp": my_grp, "dp": peer}, device_id_type=MESH,
+                ).start()
+
+            @pl.when(peer == my_dp)
+            def _():
+                brecv_s[my_dp] = bsend_s[peer]
+
     everyone = stats_s.at[pl.ds(0, n_all - 1)]
     pltpu.make_async_copy(everyone, everyone, st_recv).wait()
     every_count = stats_s[...]
@@ -161,7 +193,6 @@
         split_s[at, :LANES] = high
         split_s[at, LANES:] = (loss - high.astype(F32)).astype(BF16)
 
-    my_chunk = my_dp // group
     for i in range(n_chunks):
         c = jnp.where(my_chunk < n_chunks // 2, n_chunks - 1 - i, i)
         at = pl.ds(pl.multiple_of(c * chunk, chunk), chunk)
@@ -182,43 +213,6 @@
             @pl.when(peer == my_dp)
             def _():
                 pltpu.make_async_copy(src, dst, own_sem).start()
-
-    sub = lax.broadcasted_iota(jnp.int32, (8, LANES), 0)
-    pieces = []
-    for t in range(tiles):
-        at = slice(t * LANES, (t + 1) * LANES)
-        block = lax.dot_general(
-            jnp.ones((8, 2 * LANES), BF16), split_s[at, :], NT, preferred_element_type=F32
-        ) / jnp.maximum(block_counts[t], 1.0)
-        high = block.astype(BF16).astype(F32)
-        middle = (block - high).astype(BF16).astype(F32)
-        low = block - high - middle
-        piece = jnp.where(sub == 0, high, jnp.where(sub == 1, middle, jnp.where(sub == 2, low, 0.0)))
-        pieces.append(piece.astype(BF16))
-    blocks = jnp.concatenate(pieces, axis=1)
-    for i in range(n_chunks):
-        c = jnp.where(my_chunk < n_chunks // 2, n_chunks - 1 - i, i)
-        at = pl.ds(pl.multiple_of(c * chunk, chunk), chunk)
-        moved = jnp.sum(
-            lax.dot_general(blocks, perm_s[at, :], NT, preferred_element_type=F32), axis=0, keepdims=True
-        )
-        for q in range(group):
-            peer = c * group + q
-            part = moved[:, q * per_peer : (q + 1) * per_peer]
-            bsend_s[peer] = jnp.concatenate(
-                [part, jnp.zeros((1, LANES - per_peer), F32)], axis=1
-            )
-
-            @pl.when(peer != my_dp)
-            def _():
-                pltpu.make_async_remote_copy(
-                    src_ref=bsend_s.at[peer], dst_ref=brecv_s.at[my_dp], send_sem=blk_send,
-                    recv_sem=blk_recv, device_id={"grp": my_grp, "dp": peer}, device_id_type=MESH,
-                ).start()
-
-            @pl.when(peer == my_dp)
-            def _():
-                brecv_s[my_dp] = bsend_s[peer]
 
     own = send_s.at[pl.ds(0, per_peer)]
     pltpu.make_async_copy(own, tok_out.at[pl.ds(0, per_peer)], own_sem).wait()
@@ -234,7 +228,13 @@
         line = brecv_s[r * beside]
         for q in range(1, beside):
             line = line + pltpu.roll(brecv_s[r * beside + q], q * per_peer, 1)
-        blk_out[r : r + 1, :] = line
+        rows_in = tok_out[r * LANES : (r + 1) * LANES, :]
+        high = rows_in.astype(BF16)
+        low = (rows_in - high.astype(F32)).astype(BF16)
+        added = lax.dot_general(ones[:8], high, NT, preferred_element_type=F32) + lax.dot_general(
+            ones[:8], low, NT, preferred_element_type=F32
+        )
+        blk_out[r : r + 1, :] = added[:1] / jnp.maximum(line, 1.0)
 
 
 def finish(tok_ref, blk_ref, tok_out, blk_out, sem):

time: 28.9 us -> 25.3 us (0.88)
  the two profiles are of different devices: /device:TPU:0 before, /device:TPU:8 now
where the time goes in v4:
time: 25.3 us; the launch traced here: 25.1 us
  Pallas kernels  24.4 us (96%)
  between operations  0.64 us (3%)
    pallas_call x1, Pallas kernels, on_device(): pl.pallas_call(functools.partial(kernel, n_grp, n_dp), out_shape=(pltpu.V...  23.6 us
    pallas_call x1, Pallas kernels, on_device(): pl.pallas_call(finish, out_shape=(jax.ShapeDtypeStruct((rows, width), F32...  0.81 us

profile of v4, /device:TPU:8, one launch (start us, length us, event | category | flops | bytes accessed | tf_op | source)
XLA Modules:
  0.0 25.1 jit_solution(8787468844757153691)
XLA Ops:
  0.6 23.6 %shard_map.86 = (f32[1024,128]{1,0:T(8,128)S(1)}, f32[8,128]{1,0:T(8,128)S(1)}) custom-call(s32[8,128]{1,0:T(8,128)} %bitcast.3, s32[8,128]{1,0:T(8,128)} %bitcast.4, s32[1024,128]{1,0:T(8,128)} %mask_hbm.1, f32[1024,128]{1,0:T(8,128)} %ret_hbm.1, f32[1024,128]{1,0:T(8,128)} %val_hbm.1, f32[1024,128]{1,0:T(8,128)} %new_hbm.1, f32[1024,128]{1,0:T(8,128)} %prox_hbm.1), custom_call_target="tpu_custom_call" | custom-call | tf_op jit(solution)/shard_map/pallas_call | solution.py:262
  24.2 0.8 %shard_map.87 = (f32[1024,128]{1,0:T(8,128)}, f32[8,128]{1,0:T(8,128)}) custom-call(f32[1024,128]{1,0:T(8,128)S(1)} %get-tuple-element.6.tok_ref, f32[8,128]{1,0:T(8,128)S(1)} %get-tuple-element.7.blk_ref), custom_call_target="tpu_custom_call" | custom-call | tf_op jit(solution)/shard_map/pallas_call | solution.py:285

commit v5 on v4

--- a/solution.py
+++ b/solution.py
@@ -43,7 +43,7 @@
     rows = ret_s.shape[0]
     tiles = rows // LANES
     per_peer = rows // n_dp
-    group = max(1, 256 // per_peer)
+    group = max(1, 128 // per_peer)
     chunk = group * per_peer
     n_chunks = rows // chunk
 

time: 25.3 us -> 25.2 us (level)
  no operation moved by 1% of the time
where the time goes in v5:
time: 25.2 us; the launch traced here: 25 us
  Pallas kernels  24.4 us (97%)
  between operations  0.64 us (3%)
    pallas_call x1, Pallas kernels, on_device(): pl.pallas_call(functools.partial(kernel, n_grp, n_dp), out_shape=(pltpu.V...  23.6 us
    pallas_call x1, Pallas kernels, on_device(): pl.pallas_call(finish, out_shape=(jax.ShapeDtypeStruct((rows, width), F32...  0.81 us

profile of v5, /device:TPU:8, one launch (start us, length us, event | category | flops | bytes accessed | tf_op | source)
XLA Modules:
  0.0 25.0 jit_solution(17869941761960819172)
XLA Ops:
  0.6 23.6 %shard_map.86 = (f32[1024,128]{1,0:T(8,128)S(1)}, f32[8,128]{1,0:T(8,128)S(1)}) custom-call(s32[8,128]{1,0:T(8,128)} %bitcast.3, s32[8,128]{1,0:T(8,128)} %bitcast.4, s32[1024,128]{1,0:T(8,128)} %mask_hbm.1, f32[1024,128]{1,0:T(8,128)} %ret_hbm.1, f32[1024,128]{1,0:T(8,128)} %val_hbm.1, f32[1024,128]{1,0:T(8,128)} %new_hbm.1, f32[1024,128]{1,0:T(8,128)} %prox_hbm.1), custom_call_target="tpu_custom_call" | custom-call | tf_op jit(solution)/shard_map/pallas_call | solution.py:262
  24.2 0.8 %shard_map.87 = (f32[1024,128]{1,0:T(8,128)}, f32[8,128]{1,0:T(8,128)}) custom-call(f32[1024,128]{1,0:T(8,128)S(1)} %get-tuple-element.6.tok_ref, f32[8,128]{1,0:T(8,128)S(1)} %get-tuple-element.7.blk_ref), custom_call_target="tpu_custom_call" | custom-call | tf_op jit(solution)/shard_map/pallas_call | solution.py:285
